TPU v7x, 32 devices: a whole 2x2x4 slice. The times are simulated.
32 devices in a mesh: expert: 4 (over z), shard: 8 (over y, x, core).
Axes of the slice: x: 2, y: 2, z: 4, core: 2. Of those that a mesh axis runs over, the one named last changes fastest.
Arguments:
- tokens: bfloat16 [96, 6144], P('expert', 'shard'), may hold values from -6 to 6
- routes: int32 [96, 2], P('expert'), may hold values from 0 to 7, all different within a row; in each aligned block of 24 rows (0 to 23, 24 to 47, ...) at most 12 rows name the same one
- w_router: bfloat16 [6144, 8], replicated, may hold values from -0.078125 to 0.078125
- w_gate: bfloat16 [6144, 65536], P(None, ('expert', 'shard')), may hold values from -0.078125 to 0.078125
- w_up: bfloat16 [6144, 65536], P(None, ('expert', 'shard')), may hold values from -0.078125 to 0.078125
- w_down: bfloat16 [65536, 6144], P(('expert', 'shard')), may hold values from -0.125 to 0.125
Outputs:
- mixed: bfloat16 [96, 6144], P('expert', 'shard')
Inputs may be any that keep to these rules, and one draw needn't show every extreme that they name: `routes`: the two experts of a row differ; within each aligned block of 24 rows no expert is named more than 24 / 2 times, and some expert is named exactly that often.
All inputs are finite; a program needn't handle non-finite values.
Results may differ from a plain program's by a relative error of at most 0.017.
Values may be sent and summed in bfloat16 or wider, within the bound.
A program may use at most 256 MiB of HBM per device.

v0:
```python
import functools
import jax
import jax.numpy as jnp
from jax import lax
from jax.experimental import pallas as pl
from jax.experimental.pallas import tpu as pltpu
from jax.sharding import PartitionSpec as P

CAP = 16
WD_SLOTS = 3
F32 = jnp.float32
BF16 = jnp.bfloat16


def _nblock(n):
    for b in (512, 384, 256, 128):
        if n % b == 0:
            return b
    return n


def kernel(cfg, tok_hbm, routes_hbm, wr_hbm, wg_hbm, wu_hbm, wd_hbm, out_ref,
           tok, routes, wr, wg, wu, wd, bucket, xin, accg, accu, hid, ps, po, pin, sb, rin, eo,
           lpart, lin, small_sem, wg_sem, wu_sem, wd_sem, x_sem, xs_sem, l_sem, ls_sem, f_sem,
           p_sem, pss_sem, r_sem, rs_sem):
    G, S, E, T, DP, W, D = cfg
    nchip = S // 2
    rows = G * CAP
    g_me = lax.axis_index("expert")
    s_me = lax.axis_index("shard")
    core = lax.rem(s_me, 2)
    chip = s_me // 2
    partner = chip * 2 + (1 - core)
    per_chunk = 1 if DP % 128 == 0 else 2
    nchunk = S // per_chunk
    cw = per_chunk * DP

    def src_at(i):
        half = i // nchip
        k = i - half * nchip
        par = jnp.where(half == 0, core, 1 - core)
        return lax.rem(chip + k, nchip) * 2 + par

    smalls = [
        pltpu.make_async_copy(tok_hbm, tok, small_sem.at[0]),
        pltpu.make_async_copy(routes_hbm, routes, small_sem.at[1]),
        pltpu.make_async_copy(wr_hbm, wr, small_sem.at[2]),
    ]
    for c in smalls:
        c.start()

    def w_copy(i):
        s = src_at(i)
        r = pl.ds(pl.multiple_of(s * DP, 16), DP)
        return (pltpu.make_async_copy(wg_hbm.at[r, :], wg.at[i], wg_sem.at[i]),
                pltpu.make_async_copy(wu_hbm.at[r, :], wu.at[i], wu_sem.at[i]))

    def start_w(i, _):
        a, b = w_copy(i)
        a.start()
        b.start()
        return 0

    lax.fori_loop(0, S, start_w, 0)

    def wd_copy(k):
        if per_chunk == 1:
            j, second = k // 2, k % 2
            par = core if second else 1 - core
            col = (lax.rem(chip + j, nchip) * 2 + par) * DP
        else:
            col = lax.rem(chip + k, nchip) * cw
        return pltpu.make_async_copy(
            wd_hbm.at[:, pl.ds(pl.multiple_of(col, 128), cw)], wd.at[k % WD_SLOTS], wd_sem.at[k % WD_SLOTS])

    for k in range(min(WD_SLOTS, nchunk)):
        wd_copy(k).start()

    barrier = pltpu.get_barrier_semaphore()

    def greet(i, _):
        d = lax.rem(g_me * S + s_me + i, G * S)
        pl.semaphore_signal(barrier, inc=1, device_id={"expert": d // S, "shard": lax.rem(d, S)},
                            device_id_type=pl.DeviceIdType.MESH)
        return 0

    lax.fori_loop(1, G * S, greet, 0)

    for c in smalls:
        c.wait()

    lane = lax.broadcasted_iota(jnp.int32, (T, E * CAP), 1)
    lane_e, lane_slot = lane // CAP, lax.rem(lane, CAP)
    r0, r1 = routes[:, 0:1], routes[:, 1:2]
    is0, is1 = lane_e == r0, lane_e == r1
    member = jnp.where(is0 | is1, 1.0, 0.0).astype(F32)
    tri = jnp.where(lax.broadcasted_iota(jnp.int32, (T, T), 1)
                    < lax.broadcasted_iota(jnp.int32, (T, T), 0), 1.0, 0.0).astype(F32)
    rank = jnp.dot(tri, member, preferred_element_type=F32)
    place = jnp.where((is0 | is1) & (rank == lane_slot.astype(F32)), 1.0, 0.0).astype(F32)
    tokv = tok[...]
    tokf = tokv.astype(F32)
    got = lax.dot_general(place, tokf, (((0,), (0,)), ((), ())), preferred_element_type=F32)
    bucket[...] = got.astype(BF16).reshape(E, CAP, DP)

    spread = jnp.where(lax.broadcasted_iota(jnp.int32, (E * CAP, E), 0) // CAP
                       == lax.broadcasted_iota(jnp.int32, (E * CAP, E), 1), 1.0, 0.0).astype(F32)
    for s in range(S):
        @pl.when(s_me == s)
        def _(s=s):
            piece = wr[:, s * DP:(s + 1) * DP].astype(F32)
            wide = jnp.dot(spread, piece, preferred_element_type=F32).astype(BF16)
            lpart[...] = lax.dot_general(tokv, wide, (((1,), (1,)), ((), ())), preferred_element_type=F32)

    pl.semaphore_wait(barrier, G * S - 1)

    def x_local():
        e = (g_me * S + s_me) * E // (G * S)
        return pltpu.make_async_copy(
            bucket.at[e], xin.at[s_me, pl.ds(pl.multiple_of(g_me * CAP, CAP), CAP), :], x_sem.at[s_me])

    def x_remote(i):
        q = lax.rem(g_me * nchip + chip + i, G * nchip)
        g, s = q // nchip, lax.rem(q, nchip) * 2 + core
        e = (g * S + s) * E // (G * S)
        return pltpu.make_async_remote_copy(
            src_ref=bucket.at[e], dst_ref=xin.at[s_me, pl.ds(pl.multiple_of(g_me * CAP, CAP), CAP), :],
            send_sem=xs_sem, recv_sem=x_sem.at[s_me], device_id={"expert": g, "shard": s},
            device_id_type=pl.DeviceIdType.MESH)

    x_local().start()

    def x_start(i, _):
        x_remote(i).start()
        return 0

    lax.fori_loop(1, G * nchip, x_start, 0)

    def l_copy(i):
        return pltpu.make_async_remote_copy(
            src_ref=lpart, dst_ref=lin.at[s_me], send_sem=ls_sem, recv_sem=l_sem,
            device_id={"expert": g_me, "shard": lax.rem(s_me + i, S)},
            device_id_type=pl.DeviceIdType.MESH)

    def l_start(i, _):
        l_copy(i).start()
        return 0

    lax.fori_loop(1, S, l_start, 0)

    def forward(s):
        return pltpu.make_async_remote_copy(
            src_ref=xin.at[s], dst_ref=xin.at[s], send_sem=f_sem, recv_sem=x_sem.at[s],
            device_id={"expert": g_me, "shard": partner}, device_id_type=pl.DeviceIdType.MESH)

    accg[...] = jnp.zeros_like(accg)
    accu[...] = jnp.zeros_like(accu)
    nb = _nblock(W)

    def up_step(i, _):
        s = src_at(i)
        pltpu.make_async_copy(xin.at[s], xin.at[s], x_sem.at[s]).wait()

        @pl.when(i < nchip)
        def _():
            forward(s).start()

        a, b = w_copy(i)
        a.wait()
        b.wait()
        x = xin[s]
        for n in range(0, W, nb):
            accg[:, n:n + nb] += jnp.dot(x, wg[i, :, n:n + nb], preferred_element_type=F32)
            accu[:, n:n + nb] += jnp.dot(x, wu[i, :, n:n + nb], preferred_element_type=F32)
        return 0

    lax.fori_loop(0, S, up_step, 0)

    for n in range(0, W, nb):
        gate = accg[:, n:n + nb]
        hid[:, n:n + nb] = (gate / (1.0 + jnp.exp(-gate)) * accu[:, n:n + nb]).astype(BF16)

    def down(k, store):
        wd_copy(k).wait()
        slot = k % WD_SLOTS
        h = hid[...]
        cb = 256 if cw % 256 == 0 else cw
        for n in range(0, cw, cb):
            store(n, cb, jnp.dot(h, wd[slot, :, n:n + cb], preferred_element_type=F32))
        if k + WD_SLOTS < nchunk:
            wd_copy(k + WD_SLOTS).start()

    def pair_copy(j):
        return pltpu.make_async_remote_copy(
            src_ref=ps.at[j], dst_ref=pin.at[j], send_sem=pss_sem, recv_sem=p_sem.at[j],
            device_id={"expert": g_me, "shard": partner}, device_id_type=pl.DeviceIdType.MESH)

    q_me = g_me * nchip + chip

    def home(j, gi):
        g = lax.rem(g_me + gi, G)
        dchip = lax.rem(chip + j, nchip)
        src = sb.at[j, pl.ds(pl.multiple_of(g * CAP, CAP), CAP), :]
        if j == 0 and gi == 0:
            return pltpu.make_async_copy(src, rin.at[q_me], r_sem)
        return pltpu.make_async_remote_copy(
            src_ref=src, dst_ref=rin.at[q_me], send_sem=rs_sem, recv_sem=r_sem,
            device_id={"expert": g, "shard": dchip * 2 + core}, device_id_type=pl.DeviceIdType.MESH)

    def finish(j):
        pair_copy(j).wait_recv()
        sb[j] = (po[j] + pin[j].astype(F32)).astype(BF16)
        for gi in list(range(1, G)) + [0]:
            home(j, gi).start()

    for j in range(nchip):
        if per_chunk == 1:
            def to_ps(n, cb, v, j=j):
                ps[j, :, n:n + cb] = v.astype(BF16)

            def to_po(n, cb, v, j=j):
                po[j, :, n:n + cb] = v

            down(2 * j, to_ps)
            pair_copy(j).start()
            down(2 * j + 1, to_po)
        else:
            def to_both(n, cb, v, j=j):
                a, b = v[:, :DP], v[:, DP:]
                ps[j] = jnp.where(core == 0, b, a).astype(BF16)
                po[j] = jnp.where(core == 0, a, b)

            down(j, to_both)
            pair_copy(j).start()
        if per_chunk == 1:
            finish(j)
        elif j >= 1:
            finish(j - 1)
    if per_chunk != 1:
        finish(nchip - 1)

    pltpu.make_async_copy(lin.at[pl.ds(0, S - 1)], lin.at[pl.ds(0, S - 1)], l_sem).wait()
    lin[s_me] = lpart[...]
    logits = jnp.sum(lin[...], axis=0)
    p0 = jnp.sum(jnp.where(lane == r0 * CAP, logits, 0.0), axis=1, keepdims=True)
    p1 = jnp.sum(jnp.where(lane == r1 * CAP, logits, 0.0), axis=1, keepdims=True)
    first = 1.0 / (1.0 + jnp.exp(p1 - p0))
    second = 1.0 / (1.0 + jnp.exp(p0 - p1))
    combine = place * jnp.where(is0, first, second)

    pltpu.make_async_copy(rin, rin, r_sem).wait()
    nper = G * nchip // E
    for e in range(E):
        tot = rin[e * nper].astype(F32)
        for k in range(1, nper):
            tot = tot + rin[e * nper + k].astype(F32)
        eo[e * CAP:(e + 1) * CAP, :] = tot
    out_ref[...] = jnp.dot(combine, eo[...], precision=lax.Precision.HIGHEST,
                           preferred_element_type=F32).astype(BF16)

    def sent(ref, sem):
        pltpu.make_async_copy(ref, ref, sem).wait()

    sent(rin.at[pl.ds(0, G * nchip - 1)], xs_sem)
    sent(lin.at[pl.ds(0, S - 1)], ls_sem)
    sent(ps, f_sem)
    sent(ps, pss_sem)
    sent(rin.at[pl.ds(0, G * nchip - 1)], rs_sem)


def local(G, S, tokens, routes, w_router, w_gate, w_up, w_down):
    T, DP = tokens.shape
    D, E = w_router.shape
    W = w_gate.shape[1]
    nchip, rows = S // 2, G * CAP
    assert T // 2 <= CAP and S % 2 == 0 and (G * nchip) % E == 0
    cw = DP if DP % 128 == 0 else 2 * DP
    cfg = (G, S, E, T, DP, W, D)
    any_spec = pl.BlockSpec(memory_space=pl.ANY)
    dma = pltpu.SemaphoreType.DMA
    V = pltpu.VMEM
    return pl.pallas_call(
        functools.partial(kernel, cfg),
        out_shape=jax.ShapeDtypeStruct((T, DP), BF16),
        in_specs=[any_spec] * 6,
        out_specs=pl.BlockSpec(memory_space=pltpu.VMEM),
        scratch_shapes=[
            V((T, DP), BF16), V((T, 2), jnp.int32), V((E, D), BF16),
            V((S, DP, W), BF16), V((S, DP, W), BF16), V((WD_SLOTS, W, cw), BF16),
            V((E, CAP, DP), BF16), V((S, rows, DP), BF16),
            V((rows, W), F32), V((rows, W), F32), V((rows, W), BF16),
            V((nchip, rows, DP), BF16), V((nchip, rows, DP), F32), V((nchip, rows, DP), BF16),
            V((nchip, rows, DP), BF16), V((G * nchip, CAP, DP), BF16), V((E * CAP, DP), F32),
            V((T, E * CAP), F32), V((S, T, E * CAP), F32),
            dma((3,)), dma((S,)), dma((S,)), dma((WD_SLOTS,)), dma((S,)), dma, dma, dma, dma,
            dma((nchip,)), dma, dma, dma,
        ],
        compiler_params=pltpu.CompilerParams(
            collective_id=0, has_side_effects=True, vmem_limit_bytes=67043328),
    )(tokens, routes, w_router.T, w_gate, w_up, w_down)


def solution(mesh):
    return jax.shard_map(
        functools.partial(local, mesh.shape["expert"], mesh.shape["shard"]),
        mesh=mesh,
        in_specs=(
            P("expert", "shard"),
            P("expert", None),
            P(),
            P(None, ("expert", "shard")),
            P(None, ("expert", "shard")),
            P(("expert", "shard"), None),
        ),
        out_specs=P("expert", "shard"),
        check_vma=False,
    )
```

profile of v0, /device:TPU:0, one launch (start us, length us, event | category | flops | bytes accessed | tf_op | source)
XLA Modules:
  0.0 42.6 jit_solution(10533997530901921719)
XLA Ops:
  0.0 1.4 %copy.7.routes_hbm = s32[24,2]{1,0:T(8,128)} copy(s32[24,2]{0,1:T(2,128)} %param.7) | data formatting | bytes 384 | tf_op args[1]
  1.4 39.8 %shard_map.64 = bf16[24,768]{1,0:T(8,128)(2,1)} custom-call(bf16[24,768]{1,0:T(8,128)(2,1)} %tok_hbm.1, s32[24,2]{1,0:T(8,128)} %copy.7.routes_hbm, bf16[8,6144]{1,0:T(8,128)(2,1)} %bitcast.1, bf16[6144,2048]{1,0:T(8,128)(2,1)} %wg_hbm.1, bf16[6144,2048]{1,0:T(8,128)(2,1)} %wu_hbm.1, bf16[2048,6144]{1,0:T(8,128)(2,1)} %wd_hbm.1), custom_call_target="tpu_custom_call" | custom-call | tf_op jit(solution)/shard_map/pallas_call | solution.py:282
  41.2 1.4 %copy.9 = bf16[24,768]{1,0:T(8,128)(2,1)} copy(bf16[24,768]{1,0:T(8,128)(2,1)} %shard_map.64) | data formatting | bytes 73728
where the time goes:
time: 42.8 us; the launch traced here: 42.6 us
  Pallas kernels  39.8 us (93%)
  local copies, waits for them, and re-layouts  2.74 us (6%)
    pallas_call x1, Pallas kernels, local(): pl.pallas_call(functools.partial(kernel, cfg), out_shape=jax.ShapeDtypeSt...  39.8 us
    unnamed x2, local copies, waits for them, and re-layouts  2.74 us

commit v1 on v0

--- a/solution.py
+++ b/solution.py
@@ -20,7 +20,7 @@
 
 
 def kernel(cfg, tok_hbm, routes_hbm, wr_hbm, wg_hbm, wu_hbm, wd_hbm, out_ref,
-           tok, routes, wr, wg, wu, wd, bucket, xin, accg, accu, hid, ps, po, pin, sb, rin, eo,
+           tok, routes, wr, wg, wu, wd, bucket, xin, accg, accu, hid, ps, po, pin, sb, rin,
            lpart, lin, small_sem, wg_sem, wu_sem, wd_sem, x_sem, xs_sem, l_sem, ls_sem, f_sem,
            p_sem, pss_sem, r_sem, rs_sem):
     G, S, E, T, DP, W, D = cfg
@@ -36,10 +36,12 @@
     cw = per_chunk * DP
 
     def src_at(i):
-        half = i // nchip
-        k = i - half * nchip
+        k, half = i // 2, lax.rem(i, 2)
         par = jnp.where(half == 0, core, 1 - core)
         return lax.rem(chip + k, nchip) * 2 + par
+
+    def dest_chip(j):
+        return lax.rem(chip + 1 + j, nchip)
 
     smalls = [
         pltpu.make_async_copy(tok_hbm, tok, small_sem.at[0]),
@@ -67,9 +69,9 @@
         if per_chunk == 1:
             j, second = k // 2, k % 2
             par = core if second else 1 - core
-            col = (lax.rem(chip + j, nchip) * 2 + par) * DP
+            col = (dest_chip(j) * 2 + par) * DP
         else:
-            col = lax.rem(chip + k, nchip) * cw
+            col = dest_chip(k) * cw
         return pltpu.make_async_copy(
             wd_hbm.at[:, pl.ds(pl.multiple_of(col, 128), cw)], wd.at[k % WD_SLOTS], wd_sem.at[k % WD_SLOTS])
 
@@ -78,41 +80,37 @@
 
     barrier = pltpu.get_barrier_semaphore()
 
-    def greet(i, _):
-        d = lax.rem(g_me * S + s_me + i, G * S)
+    def greet(d, _):
         pl.semaphore_signal(barrier, inc=1, device_id={"expert": d // S, "shard": lax.rem(d, S)},
                             device_id_type=pl.DeviceIdType.MESH)
         return 0
 
-    lax.fori_loop(1, G * S, greet, 0)
+    def greet_core(i, _):
+        q = lax.rem(g_me * nchip + chip + i, G * nchip)
+        return greet(q * 2 + core, 0)
+
+    def greet_other(i, _):
+        return greet(g_me * S + i * 2 + 1 - core, 0)
+
+    lax.fori_loop(1, G * nchip, greet_core, 0)
+    lax.fori_loop(0, nchip, greet_other, 0)
 
     for c in smalls:
         c.wait()
 
-    lane = lax.broadcasted_iota(jnp.int32, (T, E * CAP), 1)
-    lane_e, lane_slot = lane // CAP, lax.rem(lane, CAP)
-    r0, r1 = routes[:, 0:1], routes[:, 1:2]
-    is0, is1 = lane_e == r0, lane_e == r1
-    member = jnp.where(is0 | is1, 1.0, 0.0).astype(F32)
-    tri = jnp.where(lax.broadcasted_iota(jnp.int32, (T, T), 1)
-                    < lax.broadcasted_iota(jnp.int32, (T, T), 0), 1.0, 0.0).astype(F32)
-    rank = jnp.dot(tri, member, preferred_element_type=F32)
-    place = jnp.where((is0 | is1) & (rank == lane_slot.astype(F32)), 1.0, 0.0).astype(F32)
+    ones = lambda m: jnp.where(m, 1.0, 0.0).astype(BF16)
+    io = lambda shape, d: lax.broadcasted_iota(jnp.int32, shape, d)
+    sub_e = io((E * CAP, T), 0) // CAP
+    sub_slot = lax.rem(io((E * CAP, T), 0), CAP)
+    named = (sub_e == routes[0:1, :]) | (sub_e == routes[1:2, :])
+    ahead = ones(io((T, T), 0) < io((T, T), 1))
+    rank = jnp.dot(ones(named), ahead, preferred_element_type=F32)
+    place = ones(named & (rank == sub_slot.astype(F32)))
     tokv = tok[...]
-    tokf = tokv.astype(F32)
-    got = lax.dot_general(place, tokf, (((0,), (0,)), ((), ())), preferred_element_type=F32)
+    got = jnp.dot(place, tokv, preferred_element_type=F32)
     bucket[...] = got.astype(BF16).reshape(E, CAP, DP)
 
-    spread = jnp.where(lax.broadcasted_iota(jnp.int32, (E * CAP, E), 0) // CAP
-                       == lax.broadcasted_iota(jnp.int32, (E * CAP, E), 1), 1.0, 0.0).astype(F32)
-    for s in range(S):
-        @pl.when(s_me == s)
-        def _(s=s):
-            piece = wr[:, s * DP:(s + 1) * DP].astype(F32)
-            wide = jnp.dot(spread, piece, preferred_element_type=F32).astype(BF16)
-            lpart[...] = lax.dot_general(tokv, wide, (((1,), (1,)), ((), ())), preferred_element_type=F32)
-
-    pl.semaphore_wait(barrier, G * S - 1)
+    pl.semaphore_wait(barrier, G * nchip - 1 + nchip)
 
     def x_local():
         e = (g_me * S + s_me) * E // (G * S)
@@ -120,8 +118,8 @@
             bucket.at[e], xin.at[s_me, pl.ds(pl.multiple_of(g_me * CAP, CAP), CAP), :], x_sem.at[s_me])
 
     def x_remote(i):
-        q = lax.rem(g_me * nchip + chip + i, G * nchip)
-        g, s = q // nchip, lax.rem(q, nchip) * 2 + core
+        k, gi = i // G, lax.rem(i, G)
+        g, s = lax.rem(g_me + gi, G), lax.rem(chip - k + nchip, nchip) * 2 + core
         e = (g * S + s) * E // (G * S)
         return pltpu.make_async_remote_copy(
             src_ref=bucket.at[e], dst_ref=xin.at[s_me, pl.ds(pl.multiple_of(g_me * CAP, CAP), CAP), :],
@@ -136,6 +134,15 @@
 
     lax.fori_loop(1, G * nchip, x_start, 0)
 
+    spread = ones(io((E * CAP, E), 0) // CAP == io((E * CAP, E), 1))
+    for s in range(S):
+        @pl.when(s_me == s)
+        def _(s=s):
+            piece = wr[:, s * DP:(s + 1) * DP]
+            wide = jnp.dot(spread, piece, preferred_element_type=F32).astype(BF16)
+            lpart[...] = lax.dot_general(tokv, wide, (((1,), (1,)), ((), ())), preferred_element_type=F32)
+
+
     def l_copy(i):
         return pltpu.make_async_remote_copy(
             src_ref=lpart, dst_ref=lin.at[s_me], send_sem=ls_sem, recv_sem=l_sem,
@@ -146,7 +153,6 @@
         l_copy(i).start()
         return 0
 
-    lax.fori_loop(1, S, l_start, 0)
 
     def forward(s):
         return pltpu.make_async_remote_copy(
@@ -161,7 +167,7 @@
         s = src_at(i)
         pltpu.make_async_copy(xin.at[s], xin.at[s], x_sem.at[s]).wait()
 
-        @pl.when(i < nchip)
+        @pl.when(lax.rem(i, 2) == 0)
         def _():
             forward(s).start()
 
@@ -175,6 +181,7 @@
         return 0
 
     lax.fori_loop(0, S, up_step, 0)
+    lax.fori_loop(1, S, l_start, 0)
 
     for n in range(0, W, nb):
         gate = accg[:, n:n + nb]
@@ -199,12 +206,13 @@
 
     def home(j, gi):
         g = lax.rem(g_me + gi, G)
-        dchip = lax.rem(chip + j, nchip)
+        dchip = dest_chip(j)
         src = sb.at[j, pl.ds(pl.multiple_of(g * CAP, CAP), CAP), :]
-        if j == 0 and gi == 0:
-            return pltpu.make_async_copy(src, rin.at[q_me], r_sem)
-        return pltpu.make_async_remote_copy(
-            src_ref=src, dst_ref=rin.at[q_me], send_sem=rs_sem, recv_sem=r_sem,
+        dst = rin.at[pl.ds(pl.multiple_of(q_me * CAP, CAP), CAP), :]
+        if j == nchip - 1 and gi == 0:
+            return pltpu.make_async_copy(src, dst, r_sem)
+        return pltpu.make_async_remote_copy(
+            src_ref=src, dst_ref=dst, send_sem=rs_sem, recv_sem=r_sem,
             device_id={"expert": g, "shard": dchip * 2 + core}, device_id_type=pl.DeviceIdType.MESH)
 
     def finish(j):
@@ -223,6 +231,8 @@
 
             down(2 * j, to_ps)
             pair_copy(j).start()
+            if j >= 1:
+                finish(j - 1)
             down(2 * j + 1, to_po)
         else:
             def to_both(n, cb, v, j=j):
@@ -232,40 +242,48 @@
 
             down(j, to_both)
             pair_copy(j).start()
-        if per_chunk == 1:
-            finish(j)
-        elif j >= 1:
+        if j >= 1 and per_chunk != 1:
             finish(j - 1)
-    if per_chunk != 1:
-        finish(nchip - 1)
+    finish(nchip - 1)
+
+    Q = G * nchip
+    nper = Q // E
+    eye = ones(io((T, T), 0) == io((T, T), 1))
+    rt = lax.dot_general(eye, routes[...].astype(F32).astype(BF16), (((1,), (1,)), ((), ())),
+                         preferred_element_type=F32)
+    r0, r1 = rt[:, 0:1].astype(jnp.int32), rt[:, 1:2].astype(jnp.int32)
+    lane = io((T, Q * CAP), 1)
+    lane_e, lane_slot = lane // CAP // nper, lax.rem(lane, CAP)
+    is0, is1 = lane_e == r0, lane_e == r1
+    before = ones(io((T, T), 1) < io((T, T), 0))
+    rank = jnp.dot(before, ones(is0 | is1), preferred_element_type=F32)
+    here = (is0 | is1) & (rank == lane_slot.astype(F32))
 
     pltpu.make_async_copy(lin.at[pl.ds(0, S - 1)], lin.at[pl.ds(0, S - 1)], l_sem).wait()
     lin[s_me] = lpart[...]
     logits = jnp.sum(lin[...], axis=0)
-    p0 = jnp.sum(jnp.where(lane == r0 * CAP, logits, 0.0), axis=1, keepdims=True)
-    p1 = jnp.sum(jnp.where(lane == r1 * CAP, logits, 0.0), axis=1, keepdims=True)
+    small = io((T, E * CAP), 1)
+    p0 = jnp.sum(jnp.where(small == r0 * CAP, logits, 0.0), axis=1, keepdims=True)
+    p1 = jnp.sum(jnp.where(small == r1 * CAP, logits, 0.0), axis=1, keepdims=True)
     first = 1.0 / (1.0 + jnp.exp(p1 - p0))
     second = 1.0 / (1.0 + jnp.exp(p0 - p1))
-    combine = place * jnp.where(is0, first, second)
+    combine = jnp.where(here, jnp.where(is0, first, second), 0.0)
+    high = combine.astype(BF16)
+    low = (combine - high.astype(F32)).astype(BF16)
 
     pltpu.make_async_copy(rin, rin, r_sem).wait()
-    nper = G * nchip // E
-    for e in range(E):
-        tot = rin[e * nper].astype(F32)
-        for k in range(1, nper):
-            tot = tot + rin[e * nper + k].astype(F32)
-        eo[e * CAP:(e + 1) * CAP, :] = tot
-    out_ref[...] = jnp.dot(combine, eo[...], precision=lax.Precision.HIGHEST,
-                           preferred_element_type=F32).astype(BF16)
+    back = rin[...]
+    out_ref[...] = (jnp.dot(high, back, preferred_element_type=F32)
+                    + jnp.dot(low, back, preferred_element_type=F32)).astype(BF16)
 
     def sent(ref, sem):
         pltpu.make_async_copy(ref, ref, sem).wait()
 
-    sent(rin.at[pl.ds(0, G * nchip - 1)], xs_sem)
+    sent(rin.at[pl.ds(0, (G * nchip - 1) * CAP)], xs_sem)
     sent(lin.at[pl.ds(0, S - 1)], ls_sem)
     sent(ps, f_sem)
     sent(ps, pss_sem)
-    sent(rin.at[pl.ds(0, G * nchip - 1)], rs_sem)
+    sent(rin.at[pl.ds(0, (G * nchip - 1) * CAP)], rs_sem)
 
 
 def local(G, S, tokens, routes, w_router, w_gate, w_up, w_down):
@@ -285,19 +303,19 @@
         in_specs=[any_spec] * 6,
         out_specs=pl.BlockSpec(memory_space=pltpu.VMEM),
         scratch_shapes=[
-            V((T, DP), BF16), V((T, 2), jnp.int32), V((E, D), BF16),
+            V((T, DP), BF16), V((2, T), jnp.int32), V((E, D), BF16),
             V((S, DP, W), BF16), V((S, DP, W), BF16), V((WD_SLOTS, W, cw), BF16),
             V((E, CAP, DP), BF16), V((S, rows, DP), BF16),
             V((rows, W), F32), V((rows, W), F32), V((rows, W), BF16),
             V((nchip, rows, DP), BF16), V((nchip, rows, DP), F32), V((nchip, rows, DP), BF16),
-            V((nchip, rows, DP), BF16), V((G * nchip, CAP, DP), BF16), V((E * CAP, DP), F32),
+            V((nchip, rows, DP), BF16), V((G * nchip * CAP, DP), BF16),
             V((T, E * CAP), F32), V((S, T, E * CAP), F32),
             dma((3,)), dma((S,)), dma((S,)), dma((WD_SLOTS,)), dma((S,)), dma, dma, dma, dma,
             dma((nchip,)), dma, dma, dma,
         ],
         compiler_params=pltpu.CompilerParams(
             collective_id=0, has_side_effects=True, vmem_limit_bytes=67043328),
-    )(tokens, routes, w_router.T, w_gate, w_up, w_down)
+    )(tokens, routes.T, w_router.T, w_gate, w_up, w_down)
 
 
 def solution(mesh):

time: 42.8 us -> 38.6 us (0.902)
  Pallas kernels: 39.8 us -> 37 us
  local copies, waits for them, and re-layouts: 2.74 us -> 1.39 us
    pallas_call x1, Pallas kernels: 39.8 us -> 37 us  [local(): pl.pallas_call(functools.partial(kernel, cfg), out_shape=jax.ShapeDtypeSt...]
    unnamed x2 -> x1, local copies, waits for them, and re-layouts: 2.74 us -> 1.39 us
where the time goes in v1:
time: 38.6 us; the launch traced here: 38.4 us
  Pallas kernels  37 us (96%)
  local copies, waits for them, and re-layouts  1.39 us (4%)
    pallas_call x1, Pallas kernels, local(): pl.pallas_call(functools.partial(kernel, cfg), out_shape=jax.ShapeDtypeSt...  37 us
    unnamed x1, local copies, waits for them, and re-layouts  1.39 us

profile of v1, /device:TPU:0, one launch (start us, length us, event | category | flops | bytes accessed | tf_op | source)
XLA Modules:
  0.0 38.4 jit_solution(1937048183082694246)
XLA Ops:
  0.0 37.0 %shard_map.64 = bf16[24,768]{1,0:T(8,128)(2,1)} custom-call(bf16[24,768]{1,0:T(8,128)(2,1)} %tok_hbm.1, s32[2,24]{1,0:T(2,128)} %bitcast.3, bf16[8,6144]{1,0:T(8,128)(2,1)} %bitcast.2, bf16[6144,2048]{1,0:T(8,128)(2,1)} %wg_hbm.1, bf16[6144,2048]{1,0:T(8,128)(2,1)} %wu_hbm.1, bf16[2048,6144]{1,0:T(8,128)(2,1)} %wd_hbm.1), custom_call_target="tpu_custom_call" | custom-call | tf_op jit(solution)/shard_map/pallas_call | solution.py:300
  37.0 1.4 %copy.8 = bf16[24,768]{1,0:T(8,128)(2,1)} copy(bf16[24,768]{1,0:T(8,128)(2,1)} %shard_map.64) | data formatting | bytes 73728

commit v2 on v1

--- a/solution.py
+++ b/solution.py
@@ -19,6 +19,14 @@
     return n
 
 
+def _rows(w, dp):
+    return [(r, min(dp, w - r)) for r in range(0, w, dp)]
+
+
+def _shared(nchip, S, DP, W):
+    return DP % 128 == 0 and 2 * DP <= W and nchip * len(_rows(W, DP)) <= 2 * (S - 2)
+
+
 def kernel(cfg, tok_hbm, routes_hbm, wr_hbm, wg_hbm, wu_hbm, wd_hbm, out_ref,
            tok, routes, wr, wg, wu, wd, bucket, xin, accg, accu, hid, ps, po, pin, sb, rin,
            lpart, lin, small_sem, wg_sem, wu_sem, wd_sem, x_sem, xs_sem, l_sem, ls_sem, f_sem,
@@ -26,6 +34,8 @@
     G, S, E, T, DP, W, D = cfg
     nchip = S // 2
     rows = G * CAP
+    quad = CAP // 4
+    most = -(-(T // 2) // 4)
     g_me = lax.axis_index("expert")
     s_me = lax.axis_index("shard")
     core = lax.rem(s_me, 2)
@@ -36,9 +46,8 @@
     cw = per_chunk * DP
 
     def src_at(i):
-        k, half = i // 2, lax.rem(i, 2)
-        par = jnp.where(half == 0, core, 1 - core)
-        return lax.rem(chip + k, nchip) * 2 + par
+        half = i // nchip
+        return lax.rem(chip + i - half * nchip, nchip) * 2 + 1 - half
 
     def dest_chip(j):
         return lax.rem(chip + 1 + j, nchip)
@@ -75,9 +84,38 @@
         return pltpu.make_async_copy(
             wd_hbm.at[:, pl.ds(pl.multiple_of(col, 128), cw)], wd.at[k % WD_SLOTS], wd_sem.at[k % WD_SLOTS])
 
-    for k in range(min(WD_SLOTS, nchunk)):
-        wd_copy(k).start()
-
+    shared = _shared(nchip, S, DP, W)
+    blocks = _rows(W, DP)
+    if not shared:
+        for k in range(min(WD_SLOTS, nchunk)):
+            wd_copy(k).start()
+
+    def home_of(j, r):
+        b = j * len(blocks) + r
+        return (wg, wu)[b % 2], b // 2
+
+    def block_copy(j, r, half):
+        buf, slot = home_of(j, r)
+        par = core if half else 1 - core
+        low, high = pl.multiple_of(par * DP, 128), blocks[r][0]
+        col = pl.multiple_of((dest_chip(j) * 2 + par) * DP, 128)
+        return pltpu.make_async_copy(
+            wd_hbm.at[pl.ds(high, blocks[r][1]), pl.ds(col, DP)],
+            buf.at[slot, pl.ds(0, blocks[r][1]), pl.ds(low, DP)],
+            wd_sem.at[(j * len(blocks) + r) * 2 + half])
+
+    def refill(i):
+        for b in (2 * i, 2 * i + 1):
+            if b < nchip * len(blocks):
+                for half in range(2):
+                    block_copy(b // len(blocks), b % len(blocks), half).start()
+
+    def blank(q, _):
+        for r in range(most, quad):
+            rin[q * quad + r] = jnp.zeros((4, DP), BF16)
+        return 0
+
+    lax.fori_loop(0, G * nchip, blank, 0)
     barrier = pltpu.get_barrier_semaphore()
 
     def greet(d, _):
@@ -108,21 +146,22 @@
     place = ones(named & (rank == sub_slot.astype(F32)))
     tokv = tok[...]
     got = jnp.dot(place, tokv, preferred_element_type=F32)
-    bucket[...] = got.astype(BF16).reshape(E, CAP, DP)
+    bucket[...] = got.reshape(E, quad, 4, DP).astype(BF16)
 
     pl.semaphore_wait(barrier, G * nchip - 1 + nchip)
 
     def x_local():
         e = (g_me * S + s_me) * E // (G * S)
         return pltpu.make_async_copy(
-            bucket.at[e], xin.at[s_me, pl.ds(pl.multiple_of(g_me * CAP, CAP), CAP), :], x_sem.at[s_me])
+            bucket.at[e, pl.ds(0, most)], xin.at[s_me, pl.ds(g_me * quad, most)], x_sem.at[s_me])
 
     def x_remote(i):
         k, gi = i // G, lax.rem(i, G)
         g, s = lax.rem(g_me + gi, G), lax.rem(chip - k + nchip, nchip) * 2 + core
         e = (g * S + s) * E // (G * S)
         return pltpu.make_async_remote_copy(
-            src_ref=bucket.at[e], dst_ref=xin.at[s_me, pl.ds(pl.multiple_of(g_me * CAP, CAP), CAP), :],
+            src_ref=bucket.at[e, pl.ds(0, most)],
+            dst_ref=xin.at[s_me, pl.ds(g_me * quad, most)],
             send_sem=xs_sem, recv_sem=x_sem.at[s_me], device_id={"expert": g, "shard": s},
             device_id_type=pl.DeviceIdType.MESH)
 
@@ -155,9 +194,11 @@
 
 
     def forward(s):
-        return pltpu.make_async_remote_copy(
-            src_ref=xin.at[s], dst_ref=xin.at[s], send_sem=f_sem, recv_sem=x_sem.at[s],
-            device_id={"expert": g_me, "shard": partner}, device_id_type=pl.DeviceIdType.MESH)
+        for g in range(G):
+            piece = xin.at[s, pl.ds(g * quad, most)]
+            pltpu.make_async_remote_copy(
+                src_ref=piece, dst_ref=piece, send_sem=f_sem, recv_sem=x_sem.at[s],
+                device_id={"expert": g_me, "shard": partner}, device_id_type=pl.DeviceIdType.MESH).start()
 
     accg[...] = jnp.zeros_like(accg)
     accu[...] = jnp.zeros_like(accu)
@@ -165,22 +206,41 @@
 
     def up_step(i, _):
         s = src_at(i)
-        pltpu.make_async_copy(xin.at[s], xin.at[s], x_sem.at[s]).wait()
-
-        @pl.when(lax.rem(i, 2) == 0)
+
+        def arrived(s):
+            got = xin.at[s, pl.ds(0, G * most)]
+            pltpu.make_async_copy(got, got, x_sem.at[s]).wait()
+
+        @pl.when((core == 0) & (i >= nchip - 1) & (i < S - 1))
         def _():
-            forward(s).start()
+            ahead = src_at(i + 1)
+            arrived(ahead)
+            forward(ahead)
+
+        @pl.when((core == 1) | (i < nchip))
+        def _():
+            arrived(s)
+
+        @pl.when((core == 1) & (i < nchip))
+        def _():
+            forward(s)
 
         a, b = w_copy(i)
         a.wait()
         b.wait()
-        x = xin[s]
+        x = xin[s].reshape(rows, DP)
         for n in range(0, W, nb):
             accg[:, n:n + nb] += jnp.dot(x, wg[i, :, n:n + nb], preferred_element_type=F32)
             accu[:, n:n + nb] += jnp.dot(x, wu[i, :, n:n + nb], preferred_element_type=F32)
         return 0
 
-    lax.fori_loop(0, S, up_step, 0)
+    if shared:
+        lax.fori_loop(0, 2, up_step, 0)
+        for i in range(2, S):
+            up_step(i, 0)
+            refill(i - 2)
+    else:
+        lax.fori_loop(0, S, up_step, 0)
     lax.fori_loop(1, S, l_start, 0)
 
     for n in range(0, W, nb):
@@ -207,8 +267,8 @@
     def home(j, gi):
         g = lax.rem(g_me + gi, G)
         dchip = dest_chip(j)
-        src = sb.at[j, pl.ds(pl.multiple_of(g * CAP, CAP), CAP), :]
-        dst = rin.at[pl.ds(pl.multiple_of(q_me * CAP, CAP), CAP), :]
+        src = sb.at[j, pl.ds(g * quad, most)]
+        dst = rin.at[pl.ds(q_me * quad, most)]
         if j == nchip - 1 and gi == 0:
             return pltpu.make_async_copy(src, dst, r_sem)
         return pltpu.make_async_remote_copy(
@@ -217,9 +277,35 @@
 
     def finish(j):
         pair_copy(j).wait_recv()
-        sb[j] = (po[j] + pin[j].astype(F32)).astype(BF16)
+        send_home(j)
+
+    def send_home(j):
+        sb[j] = (po[j] + pin[j].astype(F32)).reshape(G * quad, 4, DP).astype(BF16)
         for gi in list(range(1, G)) + [0]:
             home(j, gi).start()
+
+    cb = 256 if DP % 256 == 0 else 128
+    tiles = [(half, n) for half in range(2) for n in range(0, DP, cb)]
+    early = DP // cb + DP // cb % 2
+
+    def columns(j, todo):
+        for half, n in todo:
+            par = core if half else 1 - core
+            tot = None
+            for r, (high, depth) in enumerate(blocks):
+                buf, slot = home_of(j, r)
+                one = jnp.dot(hid[:, high:high + depth],
+                              buf[slot, 0:depth, pl.ds(pl.multiple_of(par * DP + n, 128), cb)],
+                              preferred_element_type=F32)
+                tot = one if tot is None else tot + one
+            if half:
+                po[j, :, n:n + cb] = tot
+            else:
+                ps[j, :, n:n + cb] = tot.astype(BF16)
+
+    def landed(j, half):
+        for r in range(len(blocks)):
+            block_copy(j, r, half).wait()
 
     for j in range(nchip):
         if per_chunk == 1:
@@ -229,11 +315,31 @@
             def to_po(n, cb, v, j=j):
                 po[j, :, n:n + cb] = v
 
-            down(2 * j, to_ps)
-            pair_copy(j).start()
-            if j >= 1:
-                finish(j - 1)
-            down(2 * j + 1, to_po)
+            if shared:
+                if j == 0:
+                    landed(0, 0)
+                    landed(0, 1)
+                last = j == nchip - 1
+                first = len(tiles) // 2 if last else early
+                if last and j > 0:
+                    landed(j, 0)
+                columns(j, tiles[:first])
+                pair_copy(j).start()
+                if j >= 1:
+                    pair_copy(j - 1).wait_recv()
+                    send_home(j - 1)
+                if j < nchip - 2:
+                    landed(j + 1, 0)
+                    landed(j + 1, 1)
+                if last and j > 0:
+                    landed(j, 1)
+                columns(j, tiles[first:])
+            else:
+                down(2 * j, to_ps)
+                pair_copy(j).start()
+                if j >= 1:
+                    finish(j - 1)
+                down(2 * j + 1, to_po)
         else:
             def to_both(n, cb, v, j=j):
                 a, b = v[:, :DP], v[:, DP:]
@@ -242,8 +348,8 @@
 
             down(j, to_both)
             pair_copy(j).start()
-        if j >= 1 and per_chunk != 1:
-            finish(j - 1)
+            if j >= 1:
+                finish(j - 1)
     finish(nchip - 1)
 
     Q = G * nchip
@@ -271,19 +377,20 @@
     high = combine.astype(BF16)
     low = (combine - high.astype(F32)).astype(BF16)
 
-    pltpu.make_async_copy(rin, rin, r_sem).wait()
-    back = rin[...]
+    got = rin.at[pl.ds(0, Q * most)]
+    pltpu.make_async_copy(got, got, r_sem).wait()
+    back = rin[...].reshape(Q * CAP, DP)
     out_ref[...] = (jnp.dot(high, back, preferred_element_type=F32)
                     + jnp.dot(low, back, preferred_element_type=F32)).astype(BF16)
 
     def sent(ref, sem):
         pltpu.make_async_copy(ref, ref, sem).wait()
 
-    sent(rin.at[pl.ds(0, (G * nchip - 1) * CAP)], xs_sem)
+    sent(rin.at[pl.ds(0, (Q - 1) * most)], xs_sem)
     sent(lin.at[pl.ds(0, S - 1)], ls_sem)
-    sent(ps, f_sem)
+    sent(xin.at[pl.ds(0, nchip), pl.ds(0, G * most)], f_sem)
     sent(ps, pss_sem)
-    sent(rin.at[pl.ds(0, (G * nchip - 1) * CAP)], rs_sem)
+    sent(rin.at[pl.ds(0, (Q - 1) * most)], rs_sem)
 
 
 def local(G, S, tokens, routes, w_router, w_gate, w_up, w_down):
@@ -293,28 +400,30 @@
     nchip, rows = S // 2, G * CAP
     assert T // 2 <= CAP and S % 2 == 0 and (G * nchip) % E == 0
     cw = DP if DP % 128 == 0 else 2 * DP
+    shared = _shared(nchip, S, DP, W)
+    nwd = 2 * nchip * len(_rows(W, DP)) if shared else WD_SLOTS
     cfg = (G, S, E, T, DP, W, D)
     any_spec = pl.BlockSpec(memory_space=pl.ANY)
     dma = pltpu.SemaphoreType.DMA
     V = pltpu.VMEM
     return pl.pallas_call(
         functools.partial(kernel, cfg),
-        out_shape=jax.ShapeDtypeStruct((T, DP), BF16),
+        out_shape=V((T, DP), BF16),
         in_specs=[any_spec] * 6,
         out_specs=pl.BlockSpec(memory_space=pltpu.VMEM),
         scratch_shapes=[
             V((T, DP), BF16), V((2, T), jnp.int32), V((E, D), BF16),
-            V((S, DP, W), BF16), V((S, DP, W), BF16), V((WD_SLOTS, W, cw), BF16),
-            V((E, CAP, DP), BF16), V((S, rows, DP), BF16),
+            V((S, DP, W), BF16), V((S, DP, W), BF16), V((1, 16, 128) if shared else (WD_SLOTS, W, cw), BF16),
+            V((E, CAP // 4, 4, DP), BF16), V((S, rows // 4, 4, DP), BF16),
             V((rows, W), F32), V((rows, W), F32), V((rows, W), BF16),
             V((nchip, rows, DP), BF16), V((nchip, rows, DP), F32), V((nchip, rows, DP), BF16),
-            V((nchip, rows, DP), BF16), V((G * nchip * CAP, DP), BF16),
+            V((nchip, rows // 4, 4, DP), BF16), V((G * nchip * CAP // 4, 4, DP), BF16),
             V((T, E * CAP), F32), V((S, T, E * CAP), F32),
-            dma((3,)), dma((S,)), dma((S,)), dma((WD_SLOTS,)), dma((S,)), dma, dma, dma, dma,
+            dma((3,)), dma((S,)), dma((S,)), dma((nwd,)), dma((S,)), dma, dma, dma, dma,
             dma((nchip,)), dma, dma, dma,
         ],
         compiler_params=pltpu.CompilerParams(
-            collective_id=0, has_side_effects=True, vmem_limit_bytes=67043328),
+            collective_id=0, has_side_effects=True, vmem_limit_bytes=63 * 1024 * 1024),
     )(tokens, routes.T, w_router.T, w_gate, w_up, w_down)
 
 

time: 38.6 us -> 33.6 us (0.87)
  Pallas kernels: 37 us -> 32.8 us
  local copies, waits for them, and re-layouts: 1.39 us -> 0.62 us
    pallas_call x1, Pallas kernels: 37 us -> 32.8 us  [local(): pl.pallas_call(functools.partial(kernel, cfg), out_shape=V((T, DP), BF16)...]
    unnamed x1, local copies, waits for them, and re-layouts: 1.39 us -> 0.62 us
where the time goes in v2:
time: 33.6 us; the launch traced here: 33.5 us
  Pallas kernels  32.8 us (98%)
  local copies, waits for them, and re-layouts  0.62 us (2%)
    pallas_call x1, Pallas kernels, local(): pl.pallas_call(functools.partial(kernel, cfg), out_shape=V((T, DP), BF16)...  32.8 us

profile of v2, /device:TPU:0, one launch (start us, length us, event | category | flops | bytes accessed | tf_op | source)
XLA Modules:
  0.0 33.5 jit_solution(16052197918859786926)
XLA Ops:
  0.0 32.8 %shard_map.64 = bf16[24,768]{1,0:T(8,128)(2,1)S(1)} custom-call(bf16[24,768]{1,0:T(8,128)(2,1)} %tok_hbm.1, s32[2,24]{1,0:T(2,128)} %bitcast.3, bf16[8,6144]{1,0:T(8,128)(2,1)} %bitcast.2, bf16[6144,2048]{1,0:T(8,128)(2,1)} %wg_hbm.1, bf16[6144,2048]{1,0:T(8,128)(2,1)} %wu_hbm.1, bf16[2048,6144]{1,0:T(8,128)(2,1)} %wd_hbm.1), custom_call_target="tpu_custom_call" | custom-call | tf_op jit(solution)/shard_map/pallas_call | solution.py:409
  32.9 0.6 %copy.8 = bf16[24,768]{1,0:T(8,128)(2,1)} copy(bf16[24,768]{1,0:T(8,128)(2,1)S(1)} %shard_map.64) | data formatting | bytes 73728
